TPU v7x, 128 devices: a whole 4x4x4 slice. The times are simulated.
128 devices in a mesh: rep: 8 (over z, y_lo), fsdp: 16 (over y_hi, x, core).
Axes of the slice: x: 4, y: 4 (y_hi: 2, y_lo: 2; y = y_hi * 2 + y_lo), z: 4, core: 2. Of those that a mesh axis runs over, the one named last changes fastest.
Arguments:
- tokens: bfloat16 [65536, 2048], P(('rep', 'fsdp')), may hold values from -6 to 6
- norm_gain: float32 [2048], replicated, may hold values from 0.5 to 1.5
- outer_params: float32 [2, 2048, 4096], P(None, 'fsdp'), may hold values from -6 to 6
- momentum: float32 [2, 2048, 4096], P(None, 'fsdp'), may hold values from -6 to 6
- deltas: bfloat16 [8, 2, 2048, 4096], P('rep', None, 'fsdp'), may hold values from -6 to 6
Outputs:
- new_params: float32 [2, 2048, 4096], P(None, 'fsdp')
- new_momentum: float32 [2, 2048, 4096], P(None, 'fsdp')
- hidden: bfloat16 [65536, 4096], P(('rep', 'fsdp'))
All inputs are finite; a program needn't handle non-finite values.
Results may differ from a plain program's by a relative error of at most 0.01.
Values may be sent and summed in bfloat16 or wider, within the bound.
A program may use at most 192 MiB of HBM per device.

v0:
```python
import functools
import math

import jax
import jax.numpy as jnp
from jax import lax
from jax.experimental import pallas as pl
from jax.experimental.pallas import tpu as pltpu
from jax.sharding import PartitionSpec as P

EPS = 1e-05
MU = 0.9
RATE = 0.7
CORES = 2
WIDTH = 256
SUM_LAG = 2
STEP_LAG = 3


def advance(params, moment, summed, groups):
    outer_grad = summed * (1.0 / groups)
    moment_next = MU * moment + outer_grad
    params_next = params - RATE * (outer_grad + MU * moment_next)
    return (params_next, moment_next)


def kernel(
    groups, shards,
    tokens, gain, params, moment, deltas,
    summed, hidden,
    full, own, part_in, peer_in, part, total, normed, p_slots, m_slots, h_slots,
    load_sem, token_sem, pm_sem, out_sem, h_sem,
    part_recv, peer_recv, total_recv, ring_recv, pair_recv,
    part_send, total_send, ring_send, pair_send,
):
    chunks, _, height, width = own.shape
    chips = shards // CORES
    half = chips // 2
    rows = normed.shape[0]
    rep = lax.axis_index("rep")
    mine = lax.axis_index("fsdp")
    core = mine % CORES
    chip = mine // CORES
    turn = half + chips - 1

    def flip(value):
        return value + (value // half) * (turn - 2 * value)

    place = flip(chip)

    def shard_at(position):
        return flip((position + chips) % chips) * CORES + core

    right, left = shard_at(place + 1), shard_at(place - 1)
    partner = chip * CORES + (1 - core)
    middle = groups // 2
    low = rep < middle
    inward = jnp.where(low, rep + 1, rep - 1)
    outward = jnp.where(low, rep - 1, rep + 1)
    at_end = (rep == 0) | (rep == groups - 1)
    at_middle = (rep == middle - 1) | (rep == middle)

    def columns(c):
        return pl.ds(pl.multiple_of(c * width, width), width)

    def block(c, which, owner):
        return full.at[c, which, pl.ds(pl.multiple_of(owner * height, height), height), :]

    def delta_load(c):
        return pltpu.make_async_copy(deltas.at[0, :, :, columns(c)], own.at[c], load_sem.at[c])

    def state_loads(c):
        slot = c % 2
        return (
            pltpu.make_async_copy(params.at[:, :, columns(c)], p_slots.at[slot], pm_sem.at[slot, 0]),
            pltpu.make_async_copy(moment.at[:, :, columns(c)], m_slots.at[slot], pm_sem.at[slot, 1]),
        )

    def part_copy(src, dst, c, recv):
        return pltpu.make_async_remote_copy(
            src_ref=src.at[c], dst_ref=dst.at[c], send_sem=part_send, recv_sem=recv.at[c],
            device_id={"rep": inward}, device_id_type=pl.DeviceIdType.MESH)

    def total_copy(c):
        return pltpu.make_async_remote_copy(
            src_ref=total.at[c], dst_ref=total.at[c], send_sem=total_send, recv_sem=total_recv.at[c],
            device_id={"rep": outward}, device_id_type=pl.DeviceIdType.MESH)

    def ring_copy(c, which, owner, hop, target):
        return pltpu.make_async_remote_copy(
            src_ref=block(c, which, owner), dst_ref=block(c, which, owner),
            send_sem=ring_send.at[which], recv_sem=ring_recv.at[c, which, hop - 1],
            device_id={"fsdp": target}, device_id_type=pl.DeviceIdType.MESH)

    def pair_copy(c, which, owner):
        return pltpu.make_async_remote_copy(
            src_ref=block(c, which, owner), dst_ref=block(c, which, owner),
            send_sem=pair_send, recv_sem=pair_recv.at[c],
            device_id={"fsdp": partner}, device_id_type=pl.DeviceIdType.MESH)

    @pl.loop(0, chunks)
    def _(c):
        delta_load(c).start()

    token_copy = pltpu.make_async_copy(tokens, normed, token_sem)
    token_copy.start()
    for copy in state_loads(0):
        copy.start()

    barrier = pltpu.get_barrier_semaphore()
    for target in (partner, left, right):
        pl.semaphore_signal(barrier, inc=1, device_id={"fsdp": target}, device_id_type=pl.DeviceIdType.MESH)
    pl.semaphore_signal(barrier, inc=1, device_id={"rep": inward}, device_id_type=pl.DeviceIdType.MESH)

    @pl.when(jnp.logical_not(at_end))
    def _():
        pl.semaphore_signal(barrier, inc=1, device_id={"rep": outward}, device_id_type=pl.DeviceIdType.MESH)
        pl.semaphore_wait(barrier, 5)

    @pl.when(at_end)
    def _():
        pl.semaphore_wait(barrier, 4)

    @pl.loop(0, chunks)
    def _(c):
        delta_load(c).wait()

        @pl.when(at_end & jnp.logical_not(at_middle))
        def _():
            part_copy(own, part_in, c, part_recv).start()

        @pl.when(at_end & at_middle)
        def _():
            part_copy(own, peer_in, c, peer_recv).start()

    token_copy.wait()
    piece = 64

    @pl.loop(0, rows // piece)
    def _(i):
        at = pl.ds(pl.multiple_of(i * piece, piece), piece)
        values = normed[at, :].astype(jnp.float32)
        scale = lax.rsqrt(jnp.mean(values * values, axis=-1, keepdims=True) + EPS)
        normed[at, :] = (values * scale * gain[...]).astype(jnp.bfloat16)

    factor = 1.0 / math.sqrt(normed.shape[1])
    last = chips - 1

    def live(c):
        return (c >= 0) & (c < chunks)

    @pl.loop(0, chunks + STEP_LAG + chips)
    def _(t):
        for hop in range(last, 0, -1):
            c = t - STEP_LAG - hop

            @pl.when(live(c))
            def _(c=c, hop=hop):
                for which, owner, target in ((0, shard_at(place - hop), right), (1, shard_at(place + hop), left)):
                    ring_copy(c, which, owner, hop, target).wait_recv()
                    if hop < last:
                        ring_copy(c, which, owner, hop + 1, target).start()
                    pair_copy(c, which, owner).start()

        u = t - STEP_LAG

        @pl.when(live(u))
        def _():
            @pl.when(jnp.logical_not(at_middle))
            def _():
                total_copy(u).wait_recv()

                @pl.when(jnp.logical_not(at_end))
                def _():
                    total_copy(u).start()

            @pl.when(u + 1 < chunks)
            def _():
                for copy in state_loads(u + 1):
                    copy.start()

            for copy in state_loads(u):
                copy.wait()
            slot = u % 2
            at = pl.ds(pl.multiple_of(mine * height, height), height)
            for which, target in ((0, right), (1, left)):
                stepped, _ = advance(
                    p_slots[slot, which], m_slots[slot, which], total[u, which].astype(jnp.float32), groups)
                full[u, which, at, :] = stepped.astype(jnp.bfloat16)
                ring_copy(u, which, mine, 1, target).start()
                pair_copy(u, which, mine).start()
            pltpu.make_async_copy(total.at[u], summed.at[:, :, columns(u)], out_sem).start()

        s = t - SUM_LAG

        @pl.when(live(s) & at_middle)
        def _():
            part_copy(part, peer_in, s, peer_recv).wait_recv()

            @pl.when(at_end)
            def _():
                total[s] = (own[s].astype(jnp.float32) + peer_in[s].astype(jnp.float32)).astype(jnp.bfloat16)

            @pl.when(jnp.logical_not(at_end))
            def _():
                total[s] = (part[s].astype(jnp.float32) + peer_in[s].astype(jnp.float32)).astype(jnp.bfloat16)
                total_copy(s).start()

        @pl.when((t < chunks) & jnp.logical_not(at_end))
        def _():
            part_copy(part, part_in, t, part_recv).wait_recv()
            part[t] = (own[t].astype(jnp.float32) + part_in[t].astype(jnp.float32)).astype(jnp.bfloat16)

            @pl.when(at_middle)
            def _():
                part_copy(part, peer_in, t, peer_recv).start()

            @pl.when(jnp.logical_not(at_middle))
            def _():
                part_copy(part, part_in, t, part_recv).start()

        c = t - STEP_LAG - chips

        @pl.when(live(c))
        def _():
            arrived = full.at[c, :, 0:chips * height, :]
            pltpu.make_async_copy(arrived, arrived, pair_recv.at[c]).wait()
            slot = c % 2

            @pl.when(c >= 2)
            def _():
                pltpu.make_async_copy(h_slots.at[slot], hidden.at[:, columns(c)], h_sem.at[slot]).wait()

            tall = rows // 2

            @pl.loop(0, 2)
            def _(i):
                at = pl.ds(pl.multiple_of(i * tall, tall), tall)
                gate = jnp.dot(normed[at, :], full[c, 0], preferred_element_type=jnp.float32) * factor
                up = jnp.dot(normed[at, :], full[c, 1], preferred_element_type=jnp.float32) * factor
                h_slots[slot, at, :] = (gate / (1.0 + jnp.exp(-gate)) * up).astype(jnp.bfloat16)

            pltpu.make_async_copy(h_slots.at[slot], hidden.at[:, columns(c)], h_sem.at[slot]).start()

    for slot in range(2):
        pltpu.make_async_copy(h_slots.at[slot], hidden.at[:, columns(0)], h_sem.at[slot]).wait()
    pltpu.make_async_copy(own, own, part_send).wait()
    pltpu.make_async_copy(total, total, out_sem).wait()

    @pl.when(jnp.logical_not(at_end))
    def _():
        pltpu.make_async_copy(total, total, total_send).wait()

    for which in range(2):
        sent = full.at[:, which, 0:last * height, :]
        pltpu.make_async_copy(sent, sent, ring_send.at[which]).wait()
    sent = full.at[:, :, 0:chips * height, :]
    pltpu.make_async_copy(sent, sent, pair_send).wait()


def solution(mesh):
    groups, shards = mesh.shape["rep"], mesh.shape["fsdp"]
    chips = shards // CORES

    def body(tokens, norm_gain, outer_params, momentum, deltas):
        rows, model = tokens.shape
        _, height, hid = outer_params.shape
        width = WIDTH
        chunks = hid // width
        bf16, f32 = jnp.bfloat16, jnp.float32
        dma = pltpu.SemaphoreType.DMA
        strip = pltpu.VMEM((chunks, 2, height, width), bf16)
        anywhere = pl.BlockSpec(memory_space=pl.ANY)
        summed, hidden = pl.pallas_call(
            functools.partial(kernel, groups, shards),
            out_shape=(
                jax.ShapeDtypeStruct(outer_params.shape, bf16),
                jax.ShapeDtypeStruct((rows, hid), bf16),
            ),
            in_specs=[anywhere, pl.BlockSpec(memory_space=pltpu.VMEM), anywhere, anywhere, anywhere],
            out_specs=(anywhere, anywhere),
            scratch_shapes=[
                pltpu.VMEM((chunks, 2, model, width), bf16),
                strip, strip, strip, strip, strip,
                pltpu.VMEM((rows, model), bf16),
                pltpu.VMEM((2, 2, height, width), f32),
                pltpu.VMEM((2, 2, height, width), f32),
                pltpu.VMEM((2, rows, width), bf16),
                dma((chunks,)), dma, dma((2, 2)), dma, dma((2,)),
                dma((chunks,)), dma((chunks,)), dma((chunks,)), dma((chunks, 2, chips - 1)), dma((chunks,)),
                dma, dma, dma((2,)), dma,
            ],
            compiler_params=pltpu.CompilerParams(
                collective_id=0, has_side_effects=True, vmem_limit_bytes=62 * 1024 * 1024),
            name="round",
        )(tokens, norm_gain.reshape(1, model), outer_params, momentum, deltas)
        new_params, new_momentum = advance(outer_params, momentum, summed.astype(f32), groups)
        return (new_params, new_momentum, hidden)

    in_specs = (
        P(("rep", "fsdp"), None),
        P(),
        P(None, "fsdp", None),
        P(None, "fsdp", None),
        P("rep", None, "fsdp", None),
    )
    out_specs = (P(None, "fsdp", None), P(None, "fsdp", None), P(("rep", "fsdp"), None))
    return jax.shard_map(body, mesh=mesh, in_specs=in_specs, out_specs=out_specs, check_vma=False)
```

profile of v0, /device:TPU:1, one launch (start us, length us, event | category | flops | bytes accessed | tf_op | source)
XLA Modules:
  0.0 331.4 jit_solution(4677690538724242615)
XLA Ops:
  0.6 319.3 %round.1 = (bf16[2,128,4096]{2,1,0:T(8,128)(2,1)}, bf16[512,4096]{1,0:T(8,128)(2,1)}) custom-call(bf16[512,2048]{1,0:T(8,128)(2,1)} %tokens.1, f32[1,2048]{1,0:T(1,128)} %bitcast.1, f32[2,128,4096]{2,1,0:T(8,128)} %params.1, f32[2,128,4096]{2,1,0:T(8,128)} %moment.1, bf16[1,2,128,4096]{3,2,1,0:T(8,128)(2,1)} %deltas.1), custom_call_target="tpu_custom_call" | custom-call | tf_op jit(solution)/shard_map/round/pallas_call | solution.py:274
  319.9 0.0 copy-start
  319.9 9.5 %multiply_subtract_fusion = (f32[2,128,4096]{2,1,0:T(8,128)}, f32[2,128,4096]{2,1,0:T(8,128)}) fusion(f32[2,128,4096]{2,1,0:T(8,128)} %params.1, bf16[2,128,4096]{2,1,0:T(8,128)(2,1)} %get-tuple-element.5, f32[2,128,4096]{2,1,0:T(8,128)} %moment.1), kind=kLoop, calls=%fused_computation | loop fusion | flops 8388608 | bytes 18874368 | tf_op jit(solution)/shard_map/sub | solution.py:23
  329.4 0.0 copy-done
  329.4 2.0 copy.9
Async XLA Ops:
  319.9 9.5 %copy-start = (bf16[512,4096]{1,0:T(8,128)(2,1)S(1)}, bf16[512,4096]{1,0:T(8,128)(2,1)}, u32[]{:S(2)}) copy-start(bf16[512,4096]{1,0:T(8,128)(2,1)} %get-tuple-element.14) | copy-start | bytes 12582916
where the time goes:
time: 332 us; the launch traced here: 331 us
  Pallas kernels  319 us (96%)
  other arithmetic  9.47 us (3%)
    pallas_call x1, Pallas kernels, body(): pl.pallas_call(functools.partial(kernel, groups, shards), out_shape=(jax....  319 us
    sub x1, other arithmetic, advance(): params_next = params - RATE * (outer_grad + MU * moment_next)  9.47 us

commit v1 on v0

v1 whole, which is shorter than its diff:
```python
import functools
import math

import jax
import jax.numpy as jnp
from jax import lax
from jax.experimental import pallas as pl
from jax.experimental.pallas import tpu as pltpu
from jax.sharding import PartitionSpec as P

EPS = 1e-05
MU = 0.9
RATE = 0.7
CORES = 2
WIDTH = 128
ZROWS = 16
AROWS = 8
LAST = 10


def advance(params, moment, summed, groups):
    outer_grad = summed * (1.0 / groups)
    moment_next = MU * moment + outer_grad
    params_next = params - RATE * (outer_grad + MU * moment_next)
    return (params_next, moment_next)


def kernel(
    groups, shards,
    tokens, gain, params, moment, deltas,
    new_params, new_moment, hidden,
    full, own, in1, fwd, in2, zsum, yin, tot, p_buf, m_buf, normed, raw, h_buf, w_out, z_out,
    load_sem, pm_sem, raw_sem, pm_out, h_sem,
    rs1_r, rs2_r, yex_r, ag1_r, ag2_r, pw_r, pz_r, zyc_r, zx1_r, zx2_r, zg1_r, zg2_r,
    x1_r, x2_r, yc0_r, yc1_r, yc2_r, yi_r, ayc_r, ax1_r, ax2_r, tok_r, hid_r,
    rs1_s, rs2_s, yex_s, ag1_s, ag2_s, pw_s, pz_s, zyc_s, zx1_s, zx2_s, zg1_s, zg2_s,
    x1_s, x2_s, yc0_s, yc1_s, yc2_s, yi_s, ayc_s, ax1_s, ax2_s, tok_s, hid_s,
):
    chunks = full.shape[0]
    tall = full.shape[6]
    rows = normed.shape[1]
    f32, bf16 = jnp.float32, jnp.bfloat16
    zr, ar = ZROWS, ZROWS + AROWS
    rep = lax.axis_index("rep")
    mine = lax.axis_index("fsdp")
    z, lo = rep // 2, rep % 2
    core = mine % CORES
    other = 1 - core
    chip = mine // CORES
    x, hi = chip % 4, chip // 4
    far = 1 - hi
    zp, zq, zo = z + 1 - 2 * (z % 2), 3 - z, (z + 2) % 4
    zmat, zrow = z // 2, z % 2
    up, down, across = (x + 1) % 4, (x + 3) % 4, (x + 2) % 4
    cut = (hi + lo) % 2

    def at(z_, lo_, hi_, x_, core_):
        return {"rep": z_ * 2 + lo_, "fsdp": (hi_ * 4 + x_) * CORES + core_}

    to_p, to_q = at(zp, lo, hi, x, core), at(zq, lo, hi, x, core)
    to_in, to_cross = at(z, 1 - lo, hi, x, core), at(z, 1 - lo, far, x, core)
    to_up, to_down = at(z, lo, hi, up, core), at(z, lo, hi, down, core)
    to_pair = at(z, lo, hi, x, other)

    def push(src, dst, send, recv, target):
        pltpu.make_async_remote_copy(
            src_ref=src, dst_ref=dst, send_sem=send, recv_sem=recv,
            device_id=target, device_id_type=pl.DeviceIdType.MESH).start()

    def same(ref, send, recv, target):
        push(ref, ref, send, recv, target)

    def drain(ref, sem):
        pltpu.make_async_copy(ref, ref, sem).wait()

    def columns(half, c):
        return pl.ds(pl.multiple_of((half * chunks + c) * WIDTH, WIDTH), WIDTH)

    def delta_load(c, half):
        return pltpu.make_async_copy(deltas.at[:, :, columns(half, c)], own.at[c, :, half], load_sem.at[c])

    def state_loads(c, half):
        return (
            pltpu.make_async_copy(params.at[:, :, columns(half, c)], p_buf.at[c, :, half], pm_sem.at[c, 0]),
            pltpu.make_async_copy(moment.at[:, :, columns(half, c)], m_buf.at[c, :, half], pm_sem.at[c, 1]),
        )

    def state_stores(c, half):
        return (
            pltpu.make_async_copy(p_buf.at[c, :, half], new_params.at[:, :, columns(half, c)], pm_out.at[0]),
            pltpu.make_async_copy(m_buf.at[c, :, half], new_moment.at[:, :, columns(half, c)], pm_out.at[1]),
        )

    @pl.loop(0, chunks)
    def _(c):
        for half in range(2):
            delta_load(c, half).start()

    raw_load = pltpu.make_async_copy(tokens, raw, raw_sem)
    raw_load.start()

    @pl.loop(0, chunks)
    def _(c):
        for half in range(2):
            for copy in state_loads(c, half):
                copy.start()

    barrier = pltpu.get_barrier_semaphore()
    peers = (to_p, to_q, to_in, to_cross, to_up, to_down, to_pair)
    for target in peers:
        pl.semaphore_signal(barrier, inc=1, device_id=target, device_id_type=pl.DeviceIdType.MESH)
    pl.semaphore_wait(barrier, len(peers))

    factor = 1.0 / math.sqrt(normed.shape[2])
    pieces = 8
    piece = rows // pieces

    def live(c):
        return (c >= 0) & (c < chunks)

    @pl.loop(0, chunks + LAST)
    def _(t):
        c9 = t - 9

        @pl.when(live(c9))
        def _(c=c9):
            drain(full.at[c, 0, 0, 0, :, :, ar:tall], yc2_r.at[c])
            same(full.at[c, cut, far, across, :, :, ar:tall], yi_s.at[2], yi_r.at[c], to_in)

        c8 = t - 8

        @pl.when(live(c8))
        def _(c=c8):
            drain(full.at[c, :, 0, 0, :, :, ar:tall], x2_r.at[c])
            same(full.at[c, cut, hi, across, :, :, ar:tall], yc2_s, yc2_r.at[c], to_cross)
            drain(full.at[c, :, :, 0, :, :, zr:ar], ax1_r.at[c, 0])
            same(full.at[c, 0, :, down, :, :, zr:ar], ax2_s.at[0], ax2_r.at[c], to_up)
            drain(full.at[c, :, :, 0, :, :, zr:ar], ax1_r.at[c, 1])
            same(full.at[c, 1, :, up, :, :, zr:ar], ax2_s.at[1], ax2_r.at[c], to_down)
            drain(full.at[c, :, :, :, 0, 0, 0:zr], zg1_r.at[c])
            for pm, pr in ((zmat, zrow), (zp // 2, zp % 2)):
                same(full.at[c, pm, :, :, 0, pr, 0:zr], zg2_s.at[0], zg2_r.at[c], to_q)
            for pm, pr in ((zmat, zrow), (zq // 2, zq % 2)):
                same(full.at[c, pm, :, :, 1, pr, 0:zr], zg2_s.at[1], zg2_r.at[c], to_p)
            drain(full.at[c, :, 0, 0, :, :, ar:tall], yc1_r.at[c])
            same(full.at[c, cut, far, down, :, :, ar:tall], yi_s.at[1], yi_r.at[c], to_in)
            same(full.at[c, cut, far, up, :, :, ar:tall], yi_s.at[1], yi_r.at[c], to_in)

        c7 = t - 7

        @pl.when(live(c7))
        def _(c=c7):
            drain(full.at[c, :, 0, 0, :, :, ar:tall], x1_r.at[c, 0])
            same(full.at[c, 0, hi, down, :, :, ar:tall], x2_s.at[0], x2_r.at[c], to_up)
            same(full.at[c, cut, hi, down, :, :, ar:tall], yc1_s, yc1_r.at[c], to_cross)
            drain(full.at[c, :, 0, 0, :, :, ar:tall], x1_r.at[c, 1])
            same(full.at[c, 1, hi, up, :, :, ar:tall], x2_s.at[1], x2_r.at[c], to_down)
            same(full.at[c, cut, hi, up, :, :, ar:tall], yc1_s, yc1_r.at[c], to_cross)
            drain(full.at[c, 0, :, 0, :, 0, 0:zr], zx2_r.at[c])
            same(full.at[c, zmat, :, :, 0, zrow, 0:zr], zg1_s.at[0], zg1_r.at[c], to_p)
            same(full.at[c, zmat, :, :, 1, zrow, 0:zr], zg1_s.at[1], zg1_r.at[c], to_q)
            drain(full.at[c, :, 0, 0, :, :, zr:ar], ayc_r.at[c])
            same(full.at[c, :, :, x, :, :, zr:ar], ax1_s.at[0], ax1_r.at[c, 0], to_up)
            same(full.at[c, :, :, x, :, :, zr:ar], ax1_s.at[1], ax1_r.at[c, 1], to_down)
            drain(full.at[c, 0, 0, 0, :, :, ar:tall], yc0_r.at[c])
            same(full.at[c, cut, far, x, :, :, ar:tall], yi_s.at[0], yi_r.at[c], to_in)

        c6 = t - 6

        @pl.when(live(c6))
        def _(c=c6):
            drain(w_out.at[c], pw_r.at[c])
            same(full.at[c, :, hi, x, :, :, ar:tall], x1_s.at[0], x1_r.at[c, 0], to_up)
            same(full.at[c, :, hi, x, :, :, ar:tall], x1_s.at[1], x1_r.at[c, 1], to_down)
            same(full.at[c, :, hi, x, :, :, zr:ar], ayc_s, ayc_r.at[c], to_cross)
            same(full.at[c, cut, hi, x, :, :, ar:tall], yc0_s, yc0_r.at[c], to_cross)
            drain(full.at[c, 0, :, 0, :, 0, 0:zr], zx1_r.at[c, 0])
            same(full.at[c, zmat, :, down, 0, zrow, 0:zr], zx2_s.at[0], zx2_r.at[c], to_up)
            drain(full.at[c, 0, :, 0, :, 0, 0:zr], zx1_r.at[c, 1])
            same(full.at[c, zmat, :, up, 1, zrow, 0:zr], zx2_s.at[1], zx2_r.at[c], to_down)

        c5 = t - 5

        @pl.when(live(c5))
        def _(c=c5):
            drain(in1.at[c], ag2_r.at[c])
            for half in range(2):
                is_mine = core == half
                for q in range(4):
                    p_next, m_next = advance(
                        p_buf[c, q, half], m_buf[c, q, half], tot[c, q, half].astype(f32), groups)
                    p_buf[c, q, half] = p_next
                    m_buf[c, q, half] = m_next
                    weights = p_next[zr:tall].astype(bf16)

                    @pl.when(is_mine)
                    def _(q=q, weights=weights):
                        full[c, q // 2, hi, x, core, q % 2, zr:tall, :] = weights

                    @pl.when(jnp.logical_not(is_mine))
                    def _(q=q, weights=weights):
                        w_out[c, q // 2, q % 2] = weights
            push(w_out.at[c], full.at[c, :, hi, x, core, :, zr:tall], pw_s, pw_r.at[c], to_pair)
            for half in range(2):
                for copy in state_stores(c, half):
                    copy.start()
            drain(full.at[c, 0, 0, 0, :, 0, 0:zr], zyc_r.at[c])
            same(full.at[c, zmat, :, x, :, zrow, 0:zr], zx1_s.at[0], zx1_r.at[c, 0], to_up)
            same(full.at[c, zmat, :, x, :, zrow, 0:zr], zx1_s.at[1], zx1_r.at[c, 1], to_down)

        c4 = t - 4

        @pl.when(live(c4))
        def _(c=c4):
            drain(zsum.at[c], ag1_r.at[c])
            for part in (z, zq):
                same(tot.at[c, part, 0], ag2_s.at[0], ag2_r.at[c], to_p)
            for part in (z, zp):
                same(tot.at[c, part, 1], ag2_s.at[1], ag2_r.at[c], to_q)
            drain(z_out.at[c], pz_r.at[c])
            same(full.at[c, zmat, hi, x, :, zrow, 0:zr], zyc_s, zyc_r.at[c], to_cross)

        c3 = t - 3

        @pl.when(live(c3))
        def _(c=c3):
            drain(yin.at[c], yex_r.at[c])
            tot[c, z] = (zsum[c].astype(f32) + yin[c].astype(f32)).astype(bf16)
            same(tot.at[c, z, 0], ag1_s.at[0], ag1_r.at[c], to_q)
            same(tot.at[c, z, 1], ag1_s.at[1], ag1_r.at[c], to_p)
            drain(p_buf.at[c], pm_sem.at[c, 0])
            drain(m_buf.at[c], pm_sem.at[c, 1])

            def early(half):
                p_next, _ = advance(
                    p_buf[c, z, half, 0:zr], m_buf[c, z, half, 0:zr], tot[c, z, half, 0:zr].astype(f32), groups)
                return p_next.astype(bf16)

            full[c, zmat, hi, x, core, zrow, 0:zr, :] = early(core)
            z_out[c] = early(other)
            push(z_out.at[c], full.at[c, zmat, hi, x, core, zrow, 0:zr], pz_s, pz_r.at[c], to_pair)

        c2 = t - 2

        @pl.when(live(c2))
        def _(c=c2):
            drain(in2.at[c], rs2_r.at[c])
            zsum[c] = (own[c, z].astype(f32) + in1[c, 0].astype(f32) + in2[c].astype(f32)).astype(bf16)
            push(zsum.at[c], yin.at[c], yex_s, yex_r.at[c], to_in)

        c1 = t - 1

        @pl.when(live(c1))
        def _(c=c1):
            drain(in1.at[c], rs1_r.at[c])
            fwd[c, 0] = (own[c, zq, 0].astype(f32) + in1[c, 1, 0].astype(f32)).astype(bf16)
            fwd[c, 1] = (own[c, zp, 1].astype(f32) + in1[c, 1, 1].astype(f32)).astype(bf16)
            push(fwd.at[c, 0], in2.at[c, 0], rs2_s.at[0], rs2_r.at[c], to_q)
            push(fwd.at[c, 1], in2.at[c, 1], rs2_s.at[1], rs2_r.at[c], to_p)

        @pl.when(live(t))
        def _(c=t):
            drain(own.at[c], load_sem.at[c])
            push(own.at[c, zp, 0], in1.at[c, 0, 0], rs1_s.at[0], rs1_r.at[c], to_p)
            push(own.at[c, zo, 0], in1.at[c, 1, 0], rs1_s.at[0], rs1_r.at[c], to_p)
            push(own.at[c, zq, 1], in1.at[c, 0, 1], rs1_s.at[1], rs1_r.at[c], to_q)
            push(own.at[c, zo, 1], in1.at[c, 1, 1], rs1_s.at[1], rs1_r.at[c], to_q)

        @pl.when(t == 0)
        def _():
            raw_load.wait()

        @pl.when(t < pieces)
        def _():
            span = pl.ds(pl.multiple_of(t * piece, piece), piece)
            values = raw[span, :].astype(f32)
            scale = lax.rsqrt(jnp.mean(values * values, axis=-1, keepdims=True) + EPS)
            normed[core, span, :] = (values * scale * gain[...]).astype(bf16)
            same(normed.at[core, span, :], tok_s, tok_r, to_pair)

        @pl.when(t == LAST)
        def _():
            drain(normed.at[0], tok_r)

        c10 = t - LAST

        @pl.when(live(c10))
        def _(c=c10):
            drain(full.at[c, :, :, 0, :, :, ar:tall], yi_r.at[c])
            drain(full.at[c, :, :, 0, :, :, zr:ar], ax2_r.at[c])
            drain(full.at[c, :, :, :, :, 0, 0:zr], zg2_r.at[c])
            depth = normed.shape[2]
            both = jnp.concatenate([full[c, 0].reshape(depth, WIDTH), full[c, 1].reshape(depth, WIDTH)], axis=1)

            @pl.loop(0, 2)
            def _(i):
                pair = jnp.dot(normed[i], both, preferred_element_type=f32) * factor
                gate, up_ = pair[:, 0:WIDTH], pair[:, WIDTH:2 * WIDTH]
                h_buf[c, i] = (gate / (1.0 + jnp.exp(-gate)) * up_).astype(bf16)

                @pl.when(i == core)
                def _():
                    pltpu.make_async_copy(h_buf.at[c, i], hidden.at[:, columns(core, c)], h_sem).start()

                @pl.when(i != core)
                def _():
                    push(h_buf.at[c, i], hidden.at[:, columns(core, c)], hid_s, hid_r, to_pair)

    own_half = h_buf.at[:, 0]
    drain(own_half, h_sem)
    drain(own_half, hid_s)
    drain(own_half, hid_r)
    drain(normed.at[0], tok_s)
    drain(p_buf, pm_out.at[0])
    drain(m_buf, pm_out.at[1])
    for i in range(2):
        drain(own.at[:, 0], rs1_s.at[i])
        drain(fwd.at[:, 0], rs2_s.at[i])
        drain(fwd.at[:, 0], ag1_s.at[i])
        drain(own.at[:, 0], ag2_s.at[i])
        drain(full.at[:, 0, :, 0, :, 0, 0:zr], zx1_s.at[i])
        drain(full.at[:, 0, :, 0, 0, 0, 0:zr], zx2_s.at[i])
        drain(full.at[:, 0, :, :, 0, 0, 0:zr], zg1_s.at[i])
        drain(full.at[:, :, :, :, 0, 0, 0:zr], zg2_s.at[i])
        drain(full.at[:, :, 0, 0, :, :, ar:tall], x1_s.at[i])
        drain(full.at[:, 0, 0, 0, :, :, ar:tall], x2_s.at[i])
        drain(full.at[:, :, :, 0, :, :, zr:ar], ax1_s.at[i])
        drain(full.at[:, 0, :, 0, :, :, zr:ar], ax2_s.at[i])
    drain(zsum, yex_s)
    drain(w_out, pw_s)
    drain(z_out, pz_s)
    drain(full.at[:, 0, 0, 0, :, 0, 0:zr], zyc_s)
    drain(full.at[:, 0, 0, 0, :, :, ar:tall], yc0_s)
    drain(full.at[:, :, 0, 0, :, :, ar:tall], yc1_s)
    drain(full.at[:, 0, 0, 0, :, :, ar:tall], yc2_s)
    drain(full.at[:, :, 0, 0, :, :, zr:ar], ayc_s)
    drain(full.at[:, 0, 0, 0, :, :, ar:tall], yi_s.at[0])
    drain(full.at[:, :, 0, 0, :, :, ar:tall], yi_s.at[1])
    drain(full.at[:, 0, 0, 0, :, :, ar:tall], yi_s.at[2])


def solution(mesh):
    groups, shards = mesh.shape["rep"], mesh.shape["fsdp"]

    def body(tokens, norm_gain, outer_params, momentum, deltas):
        rows, model = tokens.shape
        _, height, hid = outer_params.shape
        chunks = hid // (2 * WIDTH)
        tall = height // 2
        bf16, f32 = jnp.bfloat16, jnp.float32
        dma = pltpu.SemaphoreType.DMA
        anywhere = pl.BlockSpec(memory_space=pl.ANY)
        quarters = (4, tall, hid)

        def strip(*lead):
            return pltpu.VMEM((chunks, *lead, tall, WIDTH), bf16)

        each, two = dma((chunks,)), dma((chunks, 2))
        new_params, new_momentum, hidden = pl.pallas_call(
            functools.partial(kernel, groups, shards),
            out_shape=(
                jax.ShapeDtypeStruct(quarters, f32),
                jax.ShapeDtypeStruct(quarters, f32),
                jax.ShapeDtypeStruct((rows, hid), bf16),
            ),
            in_specs=[anywhere, pl.BlockSpec(memory_space=pltpu.VMEM), anywhere, anywhere, anywhere],
            out_specs=(anywhere, anywhere, anywhere),
            scratch_shapes=[
                strip(2, 2, 4, 2, 2),
                strip(4, 2), strip(2, 2), strip(2), strip(2), strip(2), strip(2), strip(4, 2),
                pltpu.VMEM((chunks, 4, 2, tall, WIDTH), f32),
                pltpu.VMEM((chunks, 4, 2, tall, WIDTH), f32),
                pltpu.VMEM((2, rows, model), bf16),
                pltpu.VMEM((rows, model), bf16),
                pltpu.VMEM((chunks, 2, rows, WIDTH), bf16),
                pltpu.VMEM((chunks, 2, 2, tall - ZROWS, WIDTH), bf16),
                pltpu.VMEM((chunks, ZROWS, WIDTH), bf16),
                each, two, dma, dma((2,)), dma,
                each, each, each, each, each, each, each, each, two, each, each, each,
                two, each, each, each, each, each, each, two, each, dma, dma,
                dma((2,)), dma((2,)), dma, dma((2,)), dma((2,)), dma, dma,
                dma, dma((2,)), dma((2,)), dma((2,)), dma((2,)),
                dma((2,)), dma((2,)), dma, dma, dma, dma((3,)), dma, dma((2,)), dma((2,)), dma, dma,
            ],
            compiler_params=pltpu.CompilerParams(
                collective_id=0, has_side_effects=True, vmem_limit_bytes=62 * 1024 * 1024),
            name="round",
        )(
            tokens, norm_gain.reshape(1, model), outer_params.reshape(quarters), momentum.reshape(quarters),
            deltas.reshape(quarters),
        )
        return (new_params.reshape(outer_params.shape), new_momentum.reshape(momentum.shape), hidden)

    in_specs = (
        P(("rep", "fsdp"), None),
        P(),
        P(None, "fsdp", None),
        P(None, "fsdp", None),
        P("rep", None, "fsdp", None),
    )
    out_specs = (P(None, "fsdp", None), P(None, "fsdp", None), P(("rep", "fsdp"), None))
    return jax.shard_map(body, mesh=mesh, in_specs=in_specs, out_specs=out_specs, check_vma=False)
```

time: 332 us -> 144 us (0.43)
  Pallas kernels: 319 us -> 132 us
  other arithmetic: 9.47 us -> 0 us
  local copies, waits for them, and re-layouts: 2.02 us -> 10.5 us
    pallas_call x1, Pallas kernels: 319 us -> 132 us  [body(): pl.pallas_call(functools.partial(kernel, groups, shards), out_shape=(jax....]
    sub x1 -> x0, other arithmetic: 9.47 us -> none  [advance(): params_next = params - RATE * (outer_grad + MU * moment_next)]
    unnamed x3 -> x7, local copies, waits for them, and re-layouts: 2.02 us -> 10.5 us
where the time goes in v1:
time: 144 us; the launch traced here: 143 us
  Pallas kernels  132 us (92%)
  local copies, waits for them, and re-layouts  10.5 us (7%)
    pallas_call x1, Pallas kernels, body(): pl.pallas_call(functools.partial(kernel, groups, shards), out_shape=(jax....  132 us
    unnamed x7, local copies, waits for them, and re-layouts  10.5 us

profile of v1, /device:TPU:1, one launch (start us, length us, event | category | flops | bytes accessed | tf_op | source)
XLA Modules:
  0.0 143.5 jit_solution(10711242206195634816)
XLA Ops:
  0.6 132.3 %round.1 = (f32[4,64,4096]{2,1,0:T(8,128)}, f32[4,64,4096]{2,1,0:T(8,128)}, bf16[512,4096]{1,0:T(8,128)(2,1)}) custom-call(bf16[512,2048]{1,0:T(8,128)(2,1)} %tokens.1, f32[1,2048]{1,0:T(1,128)} %bitcast.11, f32[4,64,4096]{2,1,0:T(8,128)} %bitcast.8, f32[4,64,4096]{2,1,0:T(8,128)} %bitcast.9, bf16[4,64,4096]{2,1,0:T(8,128)(2,1)} %bitcast.10), custom_call_target="tpu_custom_call" | custom-call | tf_op jit(solution)/shard_map/round/pallas_call | solution.py:359
  132.9 0.0 copy-start.1
  132.9 4.8 %copy.11 = f32[2,128,4096]{2,1,0:T(8,128)} copy(f32[2,128,4096]{2,1,0:T(8,128)} %bitcast.7) | data formatting | bytes 8388608
  137.8 0.0 copy-done.1
  137.8 0.0 copy-start
  137.8 2.1 %copy.12 = f32[2,128,4096]{2,1,0:T(8,128)} copy(f32[2,128,4096]{2,1,0:T(8,128)S(1)} %bitcast.6) | data formatting | bytes 8388608
  139.9 1.6 %copy-done = bf16[512,4096]{1,0:T(8,128)(2,1)S(1)} copy-done((bf16[512,4096]{1,0:T(8,128)(2,1)S(1)}, bf16[512,4096]{1,0:T(8,128)(2,1)}, u32[]{:S(2)}) %copy-start) | copy-done | bytes 4194328
  141.5 2.0 %copy.13 = bf16[512,4096]{1,0:T(8,128)(2,1)} copy(bf16[512,4096]{1,0:T(8,128)(2,1)S(1)} %copy-done) | data formatting | bytes 8388608
Async XLA Ops:
  132.9 4.8 %copy-start.1 = (f32[4,64,4096]{2,1,0:T(8,128)S(1)}, f32[4,64,4096]{2,1,0:T(8,128)}, u32[]{:S(2)}) copy-start(f32[4,64,4096]{2,1,0:T(8,128)} %get-tuple-element.7) | copy-start | bytes 12582916
  137.8 3.7 %copy-start = (bf16[512,4096]{1,0:T(8,128)(2,1)S(1)}, bf16[512,4096]{1,0:T(8,128)(2,1)}, u32[]{:S(2)}) copy-start(bf16[512,4096]{1,0:T(8,128)(2,1)} %get-tuple-element.14) | copy-start | bytes 12582916

commit v2 on v1

--- a/solution.py
+++ b/solution.py
@@ -15,7 +15,9 @@
 WIDTH = 128
 ZROWS = 16
 AROWS = 8
-LAST = 10
+LAGS = (0, 2, 4, 6, 8, 10, 12, 14, 16, 18, 20)
+LAST = LAGS[10]
+VMEM_LIMIT = 48 * 1024 * 1024
 
 
 def advance(params, moment, summed, groups):
@@ -28,9 +30,9 @@
 def kernel(
     groups, shards,
     tokens, gain, params, moment, deltas,
-    new_params, new_moment, hidden,
-    full, own, in1, fwd, in2, zsum, yin, tot, p_buf, m_buf, normed, raw, h_buf, w_out, z_out,
-    load_sem, pm_sem, raw_sem, pm_out, h_sem,
+    p_buf, m_buf, h_buf,
+    full, own, in1, fwd, in2, zsum, yin, tot, normed, raw, h_out, w_out, z_out,
+    load_sem, pm_sem, raw_sem,
     rs1_r, rs2_r, yex_r, ag1_r, ag2_r, pw_r, pz_r, zyc_r, zx1_r, zx2_r, zg1_r, zg2_r,
     x1_r, x2_r, yc0_r, yc1_r, yc2_r, yi_r, ayc_r, ax1_r, ax2_r, tok_r, hid_r,
     rs1_s, rs2_s, yex_s, ag1_s, ag2_s, pw_s, pz_s, zyc_s, zx1_s, zx2_s, zg1_s, zg2_s,
@@ -85,12 +87,6 @@
             pltpu.make_async_copy(moment.at[:, :, columns(half, c)], m_buf.at[c, :, half], pm_sem.at[c, 1]),
         )
 
-    def state_stores(c, half):
-        return (
-            pltpu.make_async_copy(p_buf.at[c, :, half], new_params.at[:, :, columns(half, c)], pm_out.at[0]),
-            pltpu.make_async_copy(m_buf.at[c, :, half], new_moment.at[:, :, columns(half, c)], pm_out.at[1]),
-        )
-
     @pl.loop(0, chunks)
     def _(c):
         for half in range(2):
@@ -120,14 +116,14 @@
 
     @pl.loop(0, chunks + LAST)
     def _(t):
-        c9 = t - 9
+        c9 = t - LAGS[9]
 
         @pl.when(live(c9))
         def _(c=c9):
             drain(full.at[c, 0, 0, 0, :, :, ar:tall], yc2_r.at[c])
             same(full.at[c, cut, far, across, :, :, ar:tall], yi_s.at[2], yi_r.at[c], to_in)
 
-        c8 = t - 8
+        c8 = t - LAGS[8]
 
         @pl.when(live(c8))
         def _(c=c8):
@@ -146,7 +142,7 @@
             same(full.at[c, cut, far, down, :, :, ar:tall], yi_s.at[1], yi_r.at[c], to_in)
             same(full.at[c, cut, far, up, :, :, ar:tall], yi_s.at[1], yi_r.at[c], to_in)
 
-        c7 = t - 7
+        c7 = t - LAGS[7]
 
         @pl.when(live(c7))
         def _(c=c7):
@@ -165,7 +161,7 @@
             drain(full.at[c, 0, 0, 0, :, :, ar:tall], yc0_r.at[c])
             same(full.at[c, cut, far, x, :, :, ar:tall], yi_s.at[0], yi_r.at[c], to_in)
 
-        c6 = t - 6
+        c6 = t - LAGS[6]
 
         @pl.when(live(c6))
         def _(c=c6):
@@ -179,7 +175,7 @@
             drain(full.at[c, 0, :, 0, :, 0, 0:zr], zx1_r.at[c, 1])
             same(full.at[c, zmat, :, up, 1, zrow, 0:zr], zx2_s.at[1], zx2_r.at[c], to_down)
 
-        c5 = t - 5
+        c5 = t - LAGS[5]
 
         @pl.when(live(c5))
         def _(c=c5):
@@ -201,14 +197,11 @@
                     def _(q=q, weights=weights):
                         w_out[c, q // 2, q % 2] = weights
             push(w_out.at[c], full.at[c, :, hi, x, core, :, zr:tall], pw_s, pw_r.at[c], to_pair)
-            for half in range(2):
-                for copy in state_stores(c, half):
-                    copy.start()
             drain(full.at[c, 0, 0, 0, :, 0, 0:zr], zyc_r.at[c])
             same(full.at[c, zmat, :, x, :, zrow, 0:zr], zx1_s.at[0], zx1_r.at[c, 0], to_up)
             same(full.at[c, zmat, :, x, :, zrow, 0:zr], zx1_s.at[1], zx1_r.at[c, 1], to_down)
 
-        c4 = t - 4
+        c4 = t - LAGS[4]
 
         @pl.when(live(c4))
         def _(c=c4):
@@ -220,7 +213,7 @@
             drain(z_out.at[c], pz_r.at[c])
             same(full.at[c, zmat, hi, x, :, zrow, 0:zr], zyc_s, zyc_r.at[c], to_cross)
 
-        c3 = t - 3
+        c3 = t - LAGS[3]
 
         @pl.when(live(c3))
         def _(c=c3):
@@ -240,7 +233,7 @@
             z_out[c] = early(other)
             push(z_out.at[c], full.at[c, zmat, hi, x, core, zrow, 0:zr], pz_s, pz_r.at[c], to_pair)
 
-        c2 = t - 2
+        c2 = t - LAGS[2]
 
         @pl.when(live(c2))
         def _(c=c2):
@@ -248,7 +241,7 @@
             zsum[c] = (own[c, z].astype(f32) + in1[c, 0].astype(f32) + in2[c].astype(f32)).astype(bf16)
             push(zsum.at[c], yin.at[c], yex_s, yex_r.at[c], to_in)
 
-        c1 = t - 1
+        c1 = t - LAGS[1]
 
         @pl.when(live(c1))
         def _(c=c1):
@@ -296,23 +289,20 @@
             def _(i):
                 pair = jnp.dot(normed[i], both, preferred_element_type=f32) * factor
                 gate, up_ = pair[:, 0:WIDTH], pair[:, WIDTH:2 * WIDTH]
-                h_buf[c, i] = (gate / (1.0 + jnp.exp(-gate)) * up_).astype(bf16)
+                out = (gate / (1.0 + jnp.exp(-gate)) * up_).astype(bf16)
 
                 @pl.when(i == core)
                 def _():
-                    pltpu.make_async_copy(h_buf.at[c, i], hidden.at[:, columns(core, c)], h_sem).start()
+                    h_buf[core, c] = out
 
                 @pl.when(i != core)
                 def _():
-                    push(h_buf.at[c, i], hidden.at[:, columns(core, c)], hid_s, hid_r, to_pair)
-
-    own_half = h_buf.at[:, 0]
-    drain(own_half, h_sem)
-    drain(own_half, hid_s)
-    drain(own_half, hid_r)
+                    h_out[c] = out
+                    push(h_out.at[c], h_buf.at[core, c], hid_s, hid_r, to_pair)
+
+    drain(h_out, hid_s)
+    drain(h_out, hid_r)
     drain(normed.at[0], tok_s)
-    drain(p_buf, pm_out.at[0])
-    drain(m_buf, pm_out.at[1])
     for i in range(2):
         drain(own.at[:, 0], rs1_s.at[i])
         drain(fwd.at[:, 0], rs2_s.at[i])
@@ -339,6 +329,27 @@
     drain(full.at[:, 0, 0, 0, :, :, ar:tall], yi_s.at[2])
 
 
+def settle(p_buf, m_buf, h_buf, new_params, new_moment, hidden, sems):
+    _, chunks, _, _ = h_buf.shape
+
+    def copies(half, c):
+        at = pl.ds(pl.multiple_of((half * chunks + c) * WIDTH, WIDTH), WIDTH)
+        return (
+            pltpu.make_async_copy(p_buf.at[c, :, half], new_params.at[:, :, at], sems.at[0]),
+            pltpu.make_async_copy(m_buf.at[c, :, half], new_moment.at[:, :, at], sems.at[1]),
+            pltpu.make_async_copy(h_buf.at[half, c], hidden.at[:, at], sems.at[2]),
+        )
+
+    for half in range(2):
+        @pl.loop(0, chunks)
+        def _(c):
+            for copy in copies(half, c):
+                copy.start()
+
+    for k, ref in enumerate((p_buf, m_buf, h_buf)):
+        pltpu.make_async_copy(ref, ref, sems.at[k]).wait()
+
+
 def solution(mesh):
     groups, shards = mesh.shape["rep"], mesh.shape["fsdp"]
 
@@ -350,32 +361,31 @@
         bf16, f32 = jnp.bfloat16, jnp.float32
         dma = pltpu.SemaphoreType.DMA
         anywhere = pl.BlockSpec(memory_space=pl.ANY)
+        inside = pl.BlockSpec(memory_space=pltpu.VMEM)
         quarters = (4, tall, hid)
 
         def strip(*lead):
             return pltpu.VMEM((chunks, *lead, tall, WIDTH), bf16)
 
         each, two = dma((chunks,)), dma((chunks, 2))
-        new_params, new_momentum, hidden = pl.pallas_call(
+        p_next, m_next, h_next = pl.pallas_call(
             functools.partial(kernel, groups, shards),
             out_shape=(
-                jax.ShapeDtypeStruct(quarters, f32),
-                jax.ShapeDtypeStruct(quarters, f32),
-                jax.ShapeDtypeStruct((rows, hid), bf16),
+                pltpu.VMEM((chunks, 4, 2, tall, WIDTH), f32),
+                pltpu.VMEM((chunks, 4, 2, tall, WIDTH), f32),
+                pltpu.VMEM((2, chunks, rows, WIDTH), bf16),
             ),
-            in_specs=[anywhere, pl.BlockSpec(memory_space=pltpu.VMEM), anywhere, anywhere, anywhere],
-            out_specs=(anywhere, anywhere, anywhere),
+            in_specs=[anywhere, inside, anywhere, anywhere, anywhere],
+            out_specs=(inside, inside, inside),
             scratch_shapes=[
                 strip(2, 2, 4, 2, 2),
                 strip(4, 2), strip(2, 2), strip(2), strip(2), strip(2), strip(2), strip(4, 2),
-                pltpu.VMEM((chunks, 4, 2, tall, WIDTH), f32),
-                pltpu.VMEM((chunks, 4, 2, tall, WIDTH), f32),
                 pltpu.VMEM((2, rows, model), bf16),
                 pltpu.VMEM((rows, model), bf16),
-                pltpu.VMEM((chunks, 2, rows, WIDTH), bf16),
+                pltpu.VMEM((chunks, rows, WIDTH), bf16),
                 pltpu.VMEM((chunks, 2, 2, tall - ZROWS, WIDTH), bf16),
                 pltpu.VMEM((chunks, ZROWS, WIDTH), bf16),
-                each, two, dma, dma((2,)), dma,
+                each, two, dma,
                 each, each, each, each, each, each, each, each, two, each, each, each,
                 two, each, each, each, each, each, each, two, each, dma, dma,
                 dma((2,)), dma((2,)), dma, dma((2,)), dma((2,)), dma, dma,
@@ -383,12 +393,25 @@
                 dma((2,)), dma((2,)), dma, dma, dma, dma((3,)), dma, dma((2,)), dma((2,)), dma, dma,
             ],
             compiler_params=pltpu.CompilerParams(
-                collective_id=0, has_side_effects=True, vmem_limit_bytes=62 * 1024 * 1024),
+                collective_id=0, has_side_effects=True, vmem_limit_bytes=VMEM_LIMIT),
             name="round",
         )(
             tokens, norm_gain.reshape(1, model), outer_params.reshape(quarters), momentum.reshape(quarters),
             deltas.reshape(quarters),
         )
+        new_params, new_momentum, hidden = pl.pallas_call(
+            settle,
+            out_shape=(
+                jax.ShapeDtypeStruct(quarters, f32),
+                jax.ShapeDtypeStruct(quarters, f32),
+                jax.ShapeDtypeStruct((rows, hid), bf16),
+            ),
+            in_specs=[inside, inside, inside],
+            out_specs=(anywhere, anywhere, anywhere),
+            scratch_shapes=[dma((3,))],
+            compiler_params=pltpu.CompilerParams(vmem_limit_bytes=4 * 1024 * 1024),
+            name="settle",
+        )(p_next, m_next, h_next)
         return (new_params.reshape(outer_params.shape), new_momentum.reshape(momentum.shape), hidden)
 
     in_specs = (

time: 144 us -> 119 us (0.83)
  Pallas kernels: 132 us -> 118 us
  local copies, waits for them, and re-layouts: 10.5 us -> 0 us
    pallas_call x1 -> x2, Pallas kernels: 132 us -> 118 us  [the longest x1 113 us: body(): pl.pallas_call(functools.partial(kernel, groups, shards), out_shape=(pltp...]
    unnamed x7 -> x0, local copies, waits for them, and re-layouts: 10.5 us -> none
where the time goes in v2:
time: 119 us; the launch traced here: 118 us
  Pallas kernels  118 us (99%)
    pallas_call x1, Pallas kernels, body(): pl.pallas_call(functools.partial(kernel, groups, shards), out_shape=(pltp...  113 us
    pallas_call x1, Pallas kernels, body(): pl.pallas_call(settle, out_shape=(jax.ShapeDtypeStruct(quarters, f32), ja...  4.51 us

profile of v2, /device:TPU:1, one launch (start us, length us, event | category | flops | bytes accessed | tf_op | source)
XLA Modules:
  0.0 118.5 jit_solution(17108969439225156509)
XLA Ops:
  0.6 113.3 %round.1 = (f32[16,4,2,64,128]{4,3,2,1,0:T(8,128)S(1)}, f32[16,4,2,64,128]{4,3,2,1,0:T(8,128)S(1)}, bf16[2,16,512,128]{3,2,1,0:T(8,128)(2,1)S(1)}) custom-call(bf16[512,2048]{1,0:T(8,128)(2,1)} %tokens.1, f32[1,2048]{1,0:T(1,128)} %bitcast.9, f32[4,64,4096]{2,1,0:T(8,128)} %bitcast.6, f32[4,64,4096]{2,1,0:T(8,128)} %bitcast.7, bf16[4,64,4096]{2,1,0:T(8,128)(2,1)} %bitcast.8), custom_call_target="tpu_custom_call" | custom-call | tf_op jit(solution)/shard_map/round/pallas_call | solution.py:371
  113.9 4.5 %settle.1 = (f32[4,64,4096]{2,1,0:T(8,128)}, f32[4,64,4096]{2,1,0:T(8,128)}, bf16[512,4096]{1,0:T(8,128)(2,1)}) custom-call(f32[16,4,2,64,128]{4,3,2,1,0:T(8,128)S(1)} %get-tuple-element.9.p_buf, f32[16,4,2,64,128]{4,3,2,1,0:T(8,128)S(1)} %get-tuple-element.10.m_buf, bf16[2,16,512,128]{3,2,1,0:T(8,128)(2,1)S(1)} %get-tuple-element.11.h_buf), custom_call_target="tpu_custom_call" | custom-call | tf_op jit(solution)/shard_map/settle/pallas_call | solution.py:402
